TPU v7x, 32 devices: a whole 2x2x4 slice. The times are simulated.
32 devices in a mesh: seq: 4 (over x, core), fsdp: 8 (over z, y).
Axes of the slice: x: 2, y: 2, z: 4, core: 2. Of those that a mesh axis runs over, the one named last changes fastest.
Arguments:
- tokens: bfloat16 [8, 1024, 2048], P('fsdp', 'seq'), may hold values from -6 to 6
- targets: bfloat16 [8, 1024, 2048], P('fsdp', 'seq'), may hold values from -6 to 6
- lengths: int32 [8], replicated, may hold values from 1 to 1024, 6144 in all
- w_qkv: float32 [2048, 3, 2048], P('fsdp', None, 'seq'), may hold values from -0.125 to 0.125
- w_out: float32 [2048, 2048], P('seq', 'fsdp'), may hold values from -1 to 1
- w_gateup: float32 [2048, 2, 8192], P('fsdp', None, 'seq'), may hold values from -0.125 to 0.125
- w_down: float32 [8192, 2048], P('seq', 'fsdp'), may hold values from -0.0625 to 0.0625
- mom_qkv: float32 [2048, 3, 2048], P('fsdp', None, 'seq'), may hold values from -0.0390625 to 0.0390625
- mom_out: float32 [2048, 2048], P('seq', 'fsdp'), may hold values from -0.0234375 to 0.0234375
- mom_gateup: float32 [2048, 2, 8192], P('fsdp', None, 'seq'), may hold values from -0.0390625 to 0.0390625
- mom_down: float32 [8192, 2048], P('seq', 'fsdp'), may hold values from -0.078125 to 0.078125
- avg_qkv: float32 [2048, 3, 2048], P('fsdp', None, 'seq'), may hold values from -0.125 to 0.125
- avg_out: float32 [2048, 2048], P('seq', 'fsdp'), may hold values from -1 to 1
- avg_gateup: float32 [2048, 2, 8192], P('fsdp', None, 'seq'), may hold values from -0.125 to 0.125
- avg_down: float32 [8192, 2048], P('seq', 'fsdp'), may hold values from -0.0625 to 0.0625
Outputs:
- output: bfloat16 [8, 1024, 2048], P('fsdp', 'seq')
- input_grad: bfloat16 [8, 1024, 2048], P('fsdp', 'seq')
- loss: float32 [], replicated
- new_qkv: float32 [2048, 3, 2048], P('fsdp', None, 'seq')
- new_out: float32 [2048, 2048], P('seq', 'fsdp')
- new_gateup: float32 [2048, 2, 8192], P('fsdp', None, 'seq')
- new_down: float32 [8192, 2048], P('seq', 'fsdp')
- newmom_qkv: float32 [2048, 3, 2048], P('fsdp', None, 'seq')
- newmom_out: float32 [2048, 2048], P('seq', 'fsdp')
- newmom_gateup: float32 [2048, 2, 8192], P('fsdp', None, 'seq')
- newmom_down: float32 [8192, 2048], P('seq', 'fsdp')
- newavg_qkv: float32 [2048, 3, 2048], P('fsdp', None, 'seq')
- newavg_out: float32 [2048, 2048], P('seq', 'fsdp')
- newavg_gateup: float32 [2048, 2, 8192], P('fsdp', None, 'seq')
- newavg_down: float32 [8192, 2048], P('seq', 'fsdp')
Inputs may be any that keep to these rules, and one draw needn't show every extreme that they name: lengths[s] valid tokens stand first in sequence s's 1024 slots, padding after; they sum to 6144 and one equals 1024.
All inputs are finite; a program needn't handle non-finite values.
Results may differ from a plain program's by a relative error of at most 0.015.
Values may be sent and summed in bfloat16 or wider, within the bound.
A program may use at most 256 MiB of HBM per device.

v0:
```python
import jax
import jax.numpy as jnp
from jax import lax
from jax.sharding import PartitionSpec as P

HD = 128
EPS = 1e-05
ROPE_BASE = 10000.0
MOMENT = 0.9
KEEP = 0.95
NEG = -1e30


def layer_norm(values):
    centred = values - jnp.mean(values, axis=-1, keepdims=True)
    factor = lax.rsqrt(jnp.mean(centred * centred, axis=-1, keepdims=True) + EPS)
    return (centred * factor, factor)


def norm_back(grad, normed, factor):
    inner = jnp.mean(grad * normed, axis=-1, keepdims=True)
    return factor * (grad - jnp.mean(grad, axis=-1, keepdims=True) - normed * inner)


def rotary(span, width):
    half = width // 2
    freq = ROPE_BASE ** (-2.0 * jnp.arange(half, dtype=jnp.float32) / width)
    angle = jnp.arange(span, dtype=jnp.float32)[:, None] * freq[None, :]
    cosine = jnp.concatenate([jnp.cos(angle), jnp.cos(angle)], axis=-1)[:, None, :]
    sine = jnp.concatenate([jnp.sin(angle), jnp.sin(angle)], axis=-1)[:, None, :]
    return (cosine, sine)


def rotate(values):
    half = values.shape[-1] // 2
    return jnp.concatenate([-values[..., half:], values[..., :half]], axis=-1)


def unrotate(values):
    half = values.shape[-1] // 2
    return jnp.concatenate([values[..., half:], -values[..., :half]], axis=-1)


def allowed_mask(first_row, block_rows, span, length):
    positions = jnp.arange(span, dtype=jnp.int32)
    query_pos = first_row + jnp.arange(block_rows, dtype=jnp.int32)
    return (positions[None, :] <= query_pos[:, None]) & (positions[None, :] < length)


def attend_forward(queries, keys_rot, values_v, length):
    span = queries.shape[0]
    block_rows = min(512, span)
    scale = queries.shape[2] ** (-0.5)

    def one_block(first_row):
        rows_q = lax.dynamic_slice_in_dim(queries, first_row, block_rows, 0)
        scores = (
            jnp.einsum("qhd,khd->hqk", rows_q, keys_rot, preferred_element_type=jnp.float32) * scale
        )
        scores = jnp.where(allowed_mask(first_row, block_rows, span, length)[None], scores, NEG)
        highest = jnp.max(scores, axis=-1, keepdims=True)
        expvals = jnp.exp(scores - highest)
        totals = jnp.sum(expvals, axis=-1, keepdims=True)
        attn_probs = (expvals / totals).astype(jnp.bfloat16)
        outs = jnp.einsum("hqk,khd->qhd", attn_probs, values_v, preferred_element_type=jnp.float32)
        return (outs, highest[..., 0] + jnp.log(totals[..., 0]))

    starts = jnp.arange(span // block_rows) * block_rows
    outs, log_totals = lax.map(one_block, starts)
    return (outs.reshape(span, queries.shape[1], queries.shape[2]), log_totals)


def attend_back(queries, keys_rot, values_v, grad_out, log_totals, length):
    span = queries.shape[0]
    block_rows = min(512, span)
    scale = queries.shape[2] ** (-0.5)
    starts = jnp.arange(span // block_rows) * block_rows

    def one_block(carry, item):
        first_row, lse_block = item
        rows_q = lax.dynamic_slice_in_dim(queries, first_row, block_rows, 0)
        rows_g = lax.dynamic_slice_in_dim(grad_out, first_row, block_rows, 0)
        scores = (
            jnp.einsum("qhd,khd->hqk", rows_q, keys_rot, preferred_element_type=jnp.float32) * scale
        )
        allowed = allowed_mask(first_row, block_rows, span, length)[None]
        attn_probs = jnp.where(allowed, jnp.exp(scores - lse_block[..., None]), 0.0)
        probs_low = attn_probs.astype(jnp.bfloat16)
        grad_values = carry[1] + jnp.einsum(
            "hqk,qhd->khd", probs_low, rows_g, preferred_element_type=jnp.float32
        )
        grad_probs = jnp.einsum(
            "qhd,khd->hqk", rows_g, values_v, preferred_element_type=jnp.float32
        )
        inner = jnp.sum(attn_probs * grad_probs, axis=-1, keepdims=True)
        grad_scores = (attn_probs * (grad_probs - inner)).astype(jnp.bfloat16)
        grad_rows = (
            jnp.einsum("hqk,khd->qhd", grad_scores, keys_rot, preferred_element_type=jnp.float32)
            * scale
        )
        grad_keys = (
            carry[0]
            + jnp.einsum("hqk,qhd->khd", grad_scores, rows_q, preferred_element_type=jnp.float32)
            * scale
        )
        return ((grad_keys, grad_values), grad_rows)

    zeros_kv = jnp.zeros(keys_rot.shape, jnp.float32)
    (grad_keys, grad_values), grad_rows = lax.scan(
        one_block, (zeros_kv, zeros_kv), (starts, log_totals)
    )
    return (grad_rows.reshape(queries.shape), grad_keys, grad_values)


def advance(weight, moment, average, grad, rate):
    moment_new = MOMENT * moment + grad
    weight_new = weight - rate * (grad + MOMENT * moment_new)
    average_new = KEEP * average + (1.0 - KEEP) * weight_new
    return (weight_new, moment_new, average_new)


def on_device(
    tokens,
    targets,
    lengths,
    w_qkv,
    w_out,
    w_gateup,
    w_down,
    mom_qkv,
    mom_out,
    mom_gateup,
    mom_down,
    avg_qkv,
    avg_out,
    avg_gateup,
    avg_down,
):
    n_shards = lax.axis_size("seq")
    shard_index = lax.axis_index("seq")
    member = lax.axis_index("fsdp")
    own_rows = tokens.shape[1]
    span = own_rows * n_shards
    head_size = HD
    heads_here = w_qkv.shape[2] // head_size
    inputs = tokens[0].astype(jnp.float32)
    target = targets[0].astype(jnp.float32)
    own_length = lax.dynamic_index_in_dim(lengths, member, 0, keepdims=False)
    count = jnp.sum(lengths).astype(jnp.float32)
    own_pos = shard_index * own_rows + jnp.arange(own_rows, dtype=jnp.int32)
    valid = (own_pos < own_length).astype(jnp.float32)[:, None]
    low_weights = (
        w_qkv.astype(jnp.bfloat16),
        w_out.astype(jnp.bfloat16),
        w_gateup.astype(jnp.bfloat16),
        w_down.astype(jnp.bfloat16),
    )
    full_qkv, full_out, full_gateup, full_down = (
        lax.all_gather(low_weights[0], "fsdp", axis=0, tiled=True),
        lax.all_gather(low_weights[1], "fsdp", axis=1, tiled=True),
        lax.all_gather(low_weights[2], "fsdp", axis=0, tiled=True),
        lax.all_gather(low_weights[3], "fsdp", axis=1, tiled=True),
    )
    normed_one, factor_one = layer_norm(inputs)
    group_one = lax.all_gather(normed_one.astype(jnp.bfloat16), "seq", axis=0, tiled=True)
    qkv_all = jnp.einsum("td,djc->tjc", group_one, full_qkv, preferred_element_type=jnp.float32)
    cosine, sine = rotary(span, head_size)
    queries = qkv_all[:, 0].reshape(span, heads_here, head_size)
    keys_pre = qkv_all[:, 1].reshape(span, heads_here, head_size)
    queries = (queries * cosine + rotate(queries) * sine).astype(jnp.bfloat16)
    keys_rot = (keys_pre * cosine + rotate(keys_pre) * sine).astype(jnp.bfloat16)
    values_v = qkv_all[:, 2].reshape(span, heads_here, head_size).astype(jnp.bfloat16)
    attended, log_totals = attend_forward(queries, keys_rot, values_v, own_length)
    attended = attended.reshape(span, heads_here * head_size).astype(jnp.bfloat16)
    attn_term = jnp.dot(attended, full_out, preferred_element_type=jnp.float32)
    middle = inputs + lax.psum_scatter(
        attn_term.astype(jnp.bfloat16), "seq", scatter_dimension=0, tiled=True
    ).astype(jnp.float32)
    normed_two, factor_two = layer_norm(middle)
    group_two = lax.all_gather(normed_two.astype(jnp.bfloat16), "seq", axis=0, tiled=True)
    gate_up = jnp.einsum("td,djf->tjf", group_two, full_gateup, preferred_element_type=jnp.float32)
    gate = gate_up[:, 0]
    up_part = gate_up[:, 1]
    hidden = (jax.nn.silu(gate) * up_part).astype(jnp.bfloat16)
    ffn_term = jnp.dot(hidden, full_down, preferred_element_type=jnp.float32)
    result = middle + lax.psum_scatter(
        ffn_term.astype(jnp.bfloat16), "seq", scatter_dimension=0, tiled=True
    ).astype(jnp.float32)
    diff = (result - target) * valid
    loss = lax.psum(jnp.sum(diff * diff), ("seq", "fsdp")) / (2.0 * count)
    grad_result = diff / count
    full_qkv, full_out, full_gateup, full_down = (
        lax.all_gather(low_weights[0], "fsdp", axis=0, tiled=True),
        lax.all_gather(low_weights[1], "fsdp", axis=1, tiled=True),
        lax.all_gather(low_weights[2], "fsdp", axis=0, tiled=True),
        lax.all_gather(low_weights[3], "fsdp", axis=1, tiled=True),
    )
    contract_rows = (((0,), (0,)), ((), ()))
    contract_cols = (((1,), (1,)), ((), ()))
    group_dy = lax.all_gather(grad_result.astype(jnp.bfloat16), "seq", axis=0, tiled=True)
    grad_hidden = lax.dot_general(
        group_dy, full_down, contract_cols, preferred_element_type=jnp.float32
    )
    grad_down = lax.dot_general(hidden, group_dy, contract_rows, preferred_element_type=jnp.float32)
    sigma = jax.nn.sigmoid(gate)
    grad_gate = grad_hidden * up_part * sigma * (1.0 + gate * (1.0 - sigma))
    grad_up = grad_hidden * gate * sigma
    grad_gu = jnp.stack([grad_gate, grad_up], axis=1).astype(jnp.bfloat16)
    normed_grad_two = jnp.einsum(
        "tjf,djf->td", grad_gu, full_gateup, preferred_element_type=jnp.float32
    )
    grad_gateup = jnp.einsum("td,tjf->djf", group_two, grad_gu, preferred_element_type=jnp.float32)
    own_grad_two = lax.psum_scatter(
        normed_grad_two.astype(jnp.bfloat16), "seq", scatter_dimension=0, tiled=True
    ).astype(jnp.float32)
    grad_middle = grad_result + norm_back(own_grad_two, normed_two, factor_two)
    group_da = lax.all_gather(grad_middle.astype(jnp.bfloat16), "seq", axis=0, tiled=True)
    grad_att = lax.dot_general(
        group_da, full_out, contract_cols, preferred_element_type=jnp.float32
    )
    grad_att = grad_att.astype(jnp.bfloat16).reshape(span, heads_here, head_size)
    grad_out = lax.dot_general(
        attended, group_da, contract_rows, preferred_element_type=jnp.float32
    )
    grad_rows, grad_keys, grad_values = attend_back(
        queries, keys_rot, values_v, grad_att, log_totals, own_length
    )
    grad_rows = grad_rows * cosine + unrotate(grad_rows * sine)
    grad_keys = grad_keys * cosine + unrotate(grad_keys * sine)
    grad_qkv_all = jnp.stack(
        [grad_rows.reshape(span, -1), grad_keys.reshape(span, -1), grad_values.reshape(span, -1)],
        axis=1,
    ).astype(jnp.bfloat16)
    normed_grad_one = jnp.einsum(
        "tjc,djc->td", grad_qkv_all, full_qkv, preferred_element_type=jnp.float32
    )
    grad_qkv = jnp.einsum(
        "td,tjc->djc", group_one, grad_qkv_all, preferred_element_type=jnp.float32
    )
    own_grad_one = lax.psum_scatter(
        normed_grad_one.astype(jnp.bfloat16), "seq", scatter_dimension=0, tiled=True
    ).astype(jnp.float32)
    grad_inputs = grad_middle + norm_back(own_grad_one, normed_one, factor_one)
    summed_qkv, summed_out, summed_gateup, summed_down = (
        lax.psum_scatter(
            grad_qkv.astype(jnp.bfloat16), "fsdp", scatter_dimension=0, tiled=True
        ).astype(jnp.float32),
        lax.psum_scatter(
            grad_out.astype(jnp.bfloat16), "fsdp", scatter_dimension=1, tiled=True
        ).astype(jnp.float32),
        lax.psum_scatter(
            grad_gateup.astype(jnp.bfloat16), "fsdp", scatter_dimension=0, tiled=True
        ).astype(jnp.float32),
        lax.psum_scatter(
            grad_down.astype(jnp.bfloat16), "fsdp", scatter_dimension=1, tiled=True
        ).astype(jnp.float32),
    )
    new_qkv, newmom_qkv, newavg_qkv = advance(w_qkv, mom_qkv, avg_qkv, summed_qkv, 2.0)
    new_out, newmom_out, newavg_out = advance(w_out, mom_out, avg_out, summed_out, 20.0)
    new_gateup, newmom_gateup, newavg_gateup = advance(
        w_gateup, mom_gateup, avg_gateup, summed_gateup, 2.0
    )
    new_down, newmom_down, newavg_down = advance(w_down, mom_down, avg_down, summed_down, 1.0)
    return (
        result.astype(jnp.bfloat16)[None],
        grad_inputs.astype(jnp.bfloat16)[None],
        loss,
        new_qkv,
        new_out,
        new_gateup,
        new_down,
        newmom_qkv,
        newmom_out,
        newmom_gateup,
        newmom_down,
        newavg_qkv,
        newavg_out,
        newavg_gateup,
        newavg_down,
    )


def solution(mesh):
    placed = (
        P("fsdp", "seq", None),
        P("fsdp", "seq", None),
        P(),
        P("fsdp", None, "seq"),
        P("seq", "fsdp"),
        P("fsdp", None, "seq"),
        P("seq", "fsdp"),
        P("fsdp", None, "seq"),
        P("seq", "fsdp"),
        P("fsdp", None, "seq"),
        P("seq", "fsdp"),
        P("fsdp", None, "seq"),
        P("seq", "fsdp"),
        P("fsdp", None, "seq"),
        P("seq", "fsdp"),
    )
    return jax.shard_map(
        on_device,
        mesh=mesh,
        in_specs=placed,
        out_specs=(
            P("fsdp", "seq", None),
            P("fsdp", "seq", None),
            P(),
            P("fsdp", None, "seq"),
            P("seq", "fsdp"),
            P("fsdp", None, "seq"),
            P("seq", "fsdp"),
            P("fsdp", None, "seq"),
            P("seq", "fsdp"),
            P("fsdp", None, "seq"),
            P("seq", "fsdp"),
            P("fsdp", None, "seq"),
            P("seq", "fsdp"),
            P("fsdp", None, "seq"),
            P("seq", "fsdp"),
        ),
        check_vma=False,
    )
```

profile of v0, /device:TPU:0, one launch (start us, length us, event | category | flops | bytes accessed | tf_op | source)
XLA Modules:
  0.0 1588.2 jit_solution(3938071013215438621)
XLA Ops:
  19.5 30.2 %all-gather.9.cloned.1.call-done = bf16[1024,2048]{1,0:T(8,128)(2,1)} async-done(((bf16[256,2048]{1,0:T(8,128)(2,1)}), bf16[1024,2048]{1,0:T(8,128)(2,1)}) %all-gather.9.cloned.1.call-update) | async-done | bytes 4194320 | tf_op jit(solution)/shard_map/all_gather | solution.py:165
  49.7 102.1 %all-gather.11.cloned.1.call-done = bf16[2048,3,512]{0,2,1:T(8,128)(2,1)} async-done(((bf16[256,3,512]{0,2,1:T(8,128)(2,1)}), bf16[2048,3,512]{0,2,1:T(8,128)(2,1)}) %all-gather.11.cloned.1.call-update) | async-done | bytes 6291472 | tf_op jit(solution)/shard_map/all_gather | solution.py:159
  180.4 24.5 %while.29 = (s32[]{:T(128)}, bf16[2,512,4,128]{3,1,2,0:T(8,128)(2,1)}, f32[2,4,512]{2,1,0:T(4,128)S(1)}, s32[2]{0:T(128)S(1)}, s32[]{:T(128)}, /*index=5*/bf16[1...) while((s32[]{:T(128)}, ...), condition=%wide.region_5.6_spmd.clone, body=%wide.region_2.5_spmd.sunk.clone | while | flops 1099955712 | bytes 35199660 | solution.py:69
  215.1 42.9 %reduce-scatter.9.cloned.1.call-done = bf16[256,2048]{1,0:T(8,128)(2,1)} async-done(((bf16[1024,2048]{1,0:T(8,128)(2,1)}), bf16[256,2048]{1,0:T(8,128)(2,1)}) %reduce-scatter.9.cloned.1.call-update) | async-done | bytes 1048592 | tf_op jit(solution)/shard_map/reduce_scatter | solution.py:176
  270.4 25.8 %all-gather.15.cloned.1.call-done = bf16[1024,2048]{1,0:T(8,128)(2,1)} async-done(((bf16[256,2048]{1,0:T(8,128)(2,1)}), bf16[1024,2048]{1,0:T(8,128)(2,1)}) %all-gather.15.cloned.1.call-update) | async-done | bytes 4194320 | tf_op jit(solution)/shard_map/all_gather | solution.py:180
  296.2 229.9 %all-gather.17.cloned.1.call-done = bf16[2048,2,2048]{2,0,1:T(8,128)(2,1)} async-done(((bf16[256,2,2048]{2,0,1:T(8,128)(2,1)}), bf16[2048,2,2048]{2,0,1:T(8,128)(2,1)}) %all-gather.17.cloned.1.call-update) | async-done | bytes 16777232 | tf_op jit(solution)/shard_map/all_gather | solution.py:161
  526.1 21.5 %fusion.39 = f32[1024,2,2048]{2,0,1:T(8,128)S(1)} fusion(bf16[2048,2,2048]{2,0,1:T(8,128)(2,1)} %all-gather.17.cloned.1.call-done, bf16[1024,2048]{1,0:T(8,128)(2,1)} %all-gather.15.cloned.1.call-done), kind=kOutput, calls=%fused_computation.67 | convolution fusion | flops 17179869184 | bytes 37748736 | tf_op jit(solution)/shard_map/td,djf->tjf/dot_general | solution.py:181
  557.2 94.6 %all-gather.19.cloned.1.call-done = bf16[2048,2048]{1,0:T(8,128)(2,1)} async-done(((bf16[2048,256]{1,0:T(8,128)(2,1)}), bf16[2048,2048]{1,0:T(8,128)(2,1)}) %all-gather.19.cloned.1.call-update) | async-done | bytes 8388624 | tf_op jit(solution)/shard_map/all_gather | solution.py:162
  651.9 13.8 convolution_convert_fusion.3
  668.2 40.4 %reduce-scatter.11.cloned.1.call-done = bf16[256,2048]{1,0:T(8,128)(2,1)} async-done(((bf16[1024,2048]{1,0:T(8,128)(2,1)}), bf16[256,2048]{1,0:T(8,128)(2,1)}) %reduce-scatter.11.cloned.1.call-update) | async-done | bytes 1048592 | tf_op jit(solution)/shard_map/reduce_scatter | solution.py:186
  711.7 34.6 %all-gather.21.cloned.1.call-done = bf16[1024,2048]{1,0:T(8,128)(2,1)} async-done(((bf16[256,2048]{1,0:T(8,128)(2,1)}), bf16[1024,2048]{1,0:T(8,128)(2,1)}) %all-gather.21.cloned.1.call-update) | async-done | bytes 4194320 | tf_op jit(solution)/shard_map/all_gather | solution.py:200
  746.2 20.5 %fusion.46 = (bf16[1024,1,2048]{2,0,1:T(8,128)(2,1)}, bf16[1024,1,2048]{2,0,1:T(8,128)(2,1)}) fusion(f32[1024,2,2048]{2,0,1:T(8,128)} %copy-done.16, bf16[1024,2048]{1,0:T(8,128)(2,1)} %all-gather.21.cloned.1.call-done, bf16[2048,2048]{1,0:T(8,128)(2,1)} %all-gather.19.cloned.1.call-done), kind=kOutput, calls=%fused_computation.76 | convolution fusion | flops 8617197568 | bytes 37748736 | tf_op jit(solution)/shard_map/dot_general | solution.py:201
  766.7 23.9 %bitcast_convert_fusion.1 = bf16[1024,2048]{1,0:T(8,128)(2,1)} fusion(bf16[2048,2,2048]{2,0,1:T(8,128)(2,1)} %all-gather.17.cloned.1.call-done, bf16[1024,1,2048]{2,0,1:T(8,128)(2,1)} %get-tuple-element.287, bf16[1024,1,2048]{2,0,1:T(8,128)(2,1)} %get-tuple-element.286), kind=kOutput, calls=%fused_computation.54 | convolution fusion | flops 17186160640 | bytes 29360128 | tf_op jit(solution)/shard_map/tjf,djf->td/dot_general | solution.py:209
  790.7 44.7 %reduce-scatter.13.cloned.1.call-done = bf16[256,2048]{1,0:T(8,128)(2,1)} async-done(((bf16[1024,2048]{1,0:T(8,128)(2,1)}), bf16[256,2048]{1,0:T(8,128)(2,1)}) %reduce-scatter.13.cloned.1.call-update) | async-done | bytes 1048592 | tf_op jit(solution)/shard_map/reduce_scatter | solution.py:213
  842.8 14.5 convolution_convert_fusion.1
  863.2 14.2 all-gather.23.cloned.1.call-done
  889.7 52.0 %while.30 = (s32[]{:T(128)}, f32[1024,4,128]{0,2,1:T(8,128)S(1)}, f32[1024,4,128]{0,2,1:T(8,128)}, f32[2,512,4,128]{3,1,2,0:T(8,128)}, s32[2]{0:T(128)S(1)}, /*i...) while((s32[]{:T(128)}, f32[1024,4,128]{0,2,1:T(8,128)S(1)}, ...), condition=%wide.region_16.17_spmd.clone.clone, body=%wide.region_14.16_spmd.clone.sunk.clone | while | flops 2719743488 | bytes 180419536 | solution.py:109
  996.9 24.7 %convolution_convert_fusion = bf16[2048,2,2048]{2,0,1:T(8,128)(2,1)} fusion(bf16[1024,1,2048]{2,0,1:T(8,128)(2,1)} %get-tuple-element.287, bf16[1024,1,2048]{2,0,1:T(8,128)(2,1)} %get-tuple-element.286, bf16[1024,2048]{1,0:T(8,128)(2,1)} %all-gather.15.cloned.1.call-done), kind=kOutput, calls=%fused_computation.49 | convolution fusion | flops 17205035008 | bytes 29360128 | tf_op jit(solution)/shard_map/td,tjf->djf/dot_general | solution.py:212
  1021.7 40.7 %psum.7 = f32[]{:T(128)} all-reduce(f32[]{:T(128)} %get-tuple-element.226), channel_id=1, replica_groups=mesh['seq'=4,'fsdp'=8] {'seq','fsdp'}, use_global_device_ids=true, to_apply=%region_21.22 | all-reduce | flops 1 | bytes 8 | tf_op jit(solution)/shard_map/psum | solution.py:190
  1068.9 31.1 %reduce-scatter.19.cloned.1.call-done = bf16[512,256]{1,0:T(8,128)(2,1)} async-done(((bf16[512,2048]{1,0:T(8,128)(2,1)}), bf16[512,256]{1,0:T(8,128)(2,1)}) %reduce-scatter.19.cloned.1.call-update) | async-done | bytes 262160 | tf_op jit(solution)/shard_map/reduce_scatter | solution.py:248
  1102.6 43.9 %reduce-scatter.15.cloned.1.call-done = bf16[256,2048]{1,0:T(8,128)(2,1)} async-done(((bf16[1024,2048]{1,0:T(8,128)(2,1)}), bf16[256,2048]{1,0:T(8,128)(2,1)}) %reduce-scatter.15.cloned.1.call-update) | async-done | bytes 1048592 | tf_op jit(solution)/shard_map/reduce_scatter | solution.py:240
  1150.4 118.1 %reduce-scatter.17.cloned.1.call-done = bf16[256,3,512]{2,0,1:T(8,128)(2,1)} async-done(((bf16[2048,3,512]{2,0,1:T(8,128)(2,1)}), bf16[256,3,512]{2,0,1:T(8,128)(2,1)}) %reduce-scatter.17.cloned.1.call-update) | async-done | bytes 786448 | tf_op jit(solution)/shard_map/reduce_scatter | solution.py:245
  1273.9 276.9 %reduce-scatter.21.cloned.1.call-done = bf16[256,2,2048]{2,0,1:T(8,128)(2,1)} async-done(((bf16[2048,2,2048]{2,0,1:T(8,128)(2,1)}), bf16[256,2,2048]{2,0,1:T(8,128)(2,1)}) %reduce-scatter.21.cloned.1.call-update) | async-done | bytes 2097168 | tf_op jit(solution)/shard_map/reduce_scatter | solution.py:251
  1550.8 13.7 fusion.44
  (262 shorter events, 260.0 us)
Async XLA Ops:
  7.2 42.5 %all-gather.9.cloned.1.call-start = ((), (), s32[]{:S(2)}) async-start(), calls=%async_computation.8 | async-start | bytes 5242880 | tf_op jit(solution)/shard_map/all_gather | solution.py:165
  12.4 139.5 %all-gather.11.cloned.1.call-start = ((), (), s32[]{:S(2)}) async-start(), calls=%async_computation.9 | async-start | bytes 7077888 | tf_op jit(solution)/shard_map/all_gather | solution.py:159
  13.6 195.1 %all-gather.13.cloned.1.call-start = ((), (), s32[]{:S(2)}) async-start(), calls=%async_computation.10 | async-start | bytes 2359296 | tf_op jit(solution)/shard_map/all_gather | solution.py:160
  14.5 243.5 %reduce-scatter.9.cloned.1.call-start = ((), (), s32[]{:S(2)}) async-start(), calls=%async_computation.11 | async-start | bytes 5242880 | tf_op jit(solution)/shard_map/reduce_scatter | solution.py:176
  204.9 10.1 copy-start.3
  215.0 81.1 %all-gather.15.cloned.1.call-start = ((), (), s32[]{:S(2)}) async-start(), calls=%async_computation.12 | async-start | bytes 5242880 | tf_op jit(solution)/shard_map/all_gather | solution.py:180
  261.6 264.5 %all-gather.17.cloned.1.call-start = ((), (), s32[]{:S(2)}) async-start(), calls=%async_computation.13 | async-start | bytes 18874368 | tf_op jit(solution)/shard_map/all_gather | solution.py:161
  267.4 384.5 %all-gather.19.cloned.1.call-start = ((), (), s32[]{:S(2)}) async-start(), calls=%async_computation.14 | async-start | bytes 9437184 | tf_op jit(solution)/shard_map/all_gather | solution.py:162
  270.3 438.2 %reduce-scatter.11.cloned.1.call-start = ((), (), s32[]{:S(2)}) async-start(), calls=%async_computation.15 | async-start | bytes 5242880 | tf_op jit(solution)/shard_map/reduce_scatter | solution.py:186
  665.6 42.9 %copy-start.17 = (bf16[1,256,2048]{2,1,0:T(8,128)(2,1)S(1)}, bf16[1,256,2048]{2,1,0:T(8,128)(2,1)}, u32[]{:S(2)}) copy-start(bf16[1,256,2048]{2,1,0:T(8,128)(2,1)} %param.20) | copy-start | bytes 3145732
  665.7 80.6 %all-gather.21.cloned.1.call-start = ((), (), s32[]{:S(2)}) async-start(), calls=%async_computation.16 | async-start | bytes 5242880 | tf_op jit(solution)/shard_map/all_gather | solution.py:200
  711.6 123.8 %reduce-scatter.13.cloned.1.call-start = ((), (), s32[]{:S(2)}) async-start(), calls=%async_computation.17 | async-start | bytes 5242880 | tf_op jit(solution)/shard_map/reduce_scatter | solution.py:213
  790.6 86.7 %all-gather.23.cloned.1.call-start = ((), (), s32[]{:S(2)}) async-start(), calls=%async_computation.18 | async-start | bytes 5242880 | tf_op jit(solution)/shard_map/all_gather | solution.py:217
  842.7 220.3 %reduce-scatter.23.cloned.1.call-start = ((), (), s32[]{:S(2)}) async-start(), calls=%async_computation.23 | async-start | bytes 9437184 | tf_op jit(solution)/shard_map/reduce_scatter | solution.py:254
  857.3 242.6 %reduce-scatter.19.cloned.1.call-start = ((), (), s32[]{:S(2)}) async-start(), calls=%async_computation.21 | async-start | bytes 2359296 | tf_op jit(solution)/shard_map/reduce_scatter | solution.py:248
  860.0 17.3 %copy-start.34 = (bf16[2,512,4,128]{3,2,1,0:T(4,128)(2,1)S(1)}, bf16[2,512,4,128]{3,2,1,0:T(4,128)(2,1)}, u32[]{:S(2)}) copy-start(bf16[2,512,4,128]{3,2,1,0:T(4,128)(2,1)} %copy.65) | copy-start | bytes 3145732
  883.3 263.2 %reduce-scatter.15.cloned.1.call-start = ((), (), s32[]{:S(2)}) async-start(), calls=%async_computation.19 | async-start | bytes 5242880 | tf_op jit(solution)/shard_map/reduce_scatter | solution.py:240
  983.9 284.5 %reduce-scatter.17.cloned.1.call-start = ((), (), s32[]{:S(2)}) async-start(), calls=%async_computation.20 | async-start | bytes 7077888 | tf_op jit(solution)/shard_map/reduce_scatter | solution.py:245
  996.9 553.9 %reduce-scatter.21.cloned.1.call-start = ((), (), s32[]{:S(2)}) async-start(), calls=%async_computation.22 | async-start | bytes 18874368 | tf_op jit(solution)/shard_map/reduce_scatter | solution.py:251
  1021.7 41.4 %copy-start.21 = (f32[2048,256]{1,0:T(8,128)S(1)}, f32[2048,256]{1,0:T(8,128)}, u32[]{:S(2)}) copy-start(f32[2048,256]{1,0:T(8,128)} %param.25) | copy-start | bytes 6291460
  1068.9 77.7 %copy-start.6 = (bf16[1,256,2048]{2,1,0:T(8,128)(2,1)S(1)}, bf16[1,256,2048]{2,1,0:T(8,128)(2,1)}, u32[]{:S(2)}) copy-start(bf16[1,256,2048]{2,1,0:T(8,128)(2,1)} %param.19) | copy-start | bytes 3145732
  1068.9 77.7 %copy-start.42 = (f32[256]{0:T(256)S(1)}, f32[256]{0:T(256)}, u32[]{:S(2)}) copy-start(f32[256]{0:T(256)} %copy-done.41) | copy-start | bytes 3076
  1068.9 77.7 %copy-start.44 = (f32[256]{0:T(256)S(1)}, f32[256]{0:T(256)}, u32[]{:S(2)}) copy-start(f32[256]{0:T(256)} %copy-done.43) | copy-start | bytes 3076
  1068.9 79.7 %copy-start.22 = (f32[256,2048]{1,0:T(8,128)S(1)}, f32[256,2048]{1,0:T(8,128)}, u32[]{:S(2)}) copy-start(f32[256,2048]{1,0:T(8,128)} %get-tuple-element.281) | copy-start | bytes 6291460
  (50 other events, 194.9 us)
Sparse Core Ops, SparseCore 0:
  12.5 37.1 all-gather.8
  52.3 99.4 all-gather.10
  154.5 48.5 all-gather.12
  215.2 42.7 reduce-scatter.8
  261.7 34.4 all-gather.14
  298.8 227.2 all-gather.16
  528.7 123.1 all-gather.18
  665.8 42.7 reduce-scatter.10
  711.7 34.4 all-gather.20
  790.8 44.5 reduce-scatter.12
  842.8 34.4 all-gather.22
  880.8 147.8 reduce-scatter.22
  1032.2 67.6 reduce-scatter.18
  1102.9 43.5 reduce-scatter.14
  1150.0 118.4 reduce-scatter.16
  1272.1 278.7 reduce-scatter.20
where the time goes:
time: 1590 us
  waiting for transfers between devices  1130 us (71%)
  matrix products  215 us (14%)
  other arithmetic  98.9 us (6%)
  local copies, waits for them, and re-layouts  78.1 us (5%)
  blocking collectives  40.7 us (3%)
  between operations  17.1 us (1%)
    reduce_scatter x1, waiting for transfers between devices, on_device(): lax.psum_scatter(grad_gateup.astype(jnp.bfloat16), 'fsdp', scatter_dimens...  277 us
    all_gather x1, waiting for transfers between devices, on_device(): lax.all_gather(low_weights[2], 'fsdp', axis=0, tiled=True)  230 us
    reduce_scatter x1, waiting for transfers between devices, on_device(): lax.psum_scatter(grad_qkv.astype(jnp.bfloat16), 'fsdp', scatter_dimension...  118 us
    all_gather x1, waiting for transfers between devices, on_device(): lax.all_gather(low_weights[0], 'fsdp', axis=0, tiled=True)  102 us
    all_gather x1, waiting for transfers between devices, on_device(): lax.all_gather(low_weights[3], 'fsdp', axis=1, tiled=True)  94.6 us
    reduce_scatter x1, waiting for transfers between devices, on_device(): lax.psum_scatter(normed_grad_two.astype(jnp.bfloat16), 'seq', scatter_dim...  44.7 us
    reduce_scatter x1, waiting for transfers between devices, on_device(): lax.psum_scatter(normed_grad_one.astype(jnp.bfloat16), 'seq', scatter_dim...  43.9 us
    reduce_scatter x1, waiting for transfers between devices, on_device(): lax.psum_scatter(attn_term.astype(jnp.bfloat16), 'seq', scatter_dimension...  42.9 us
  transfers between devices with their start and end apart: 16, of which 14 were waited for; matrix products, arithmetic and copies ran while one was open for 17% of the time, Pallas kernels for 0%

commit v1 on v0

--- a/solution.py
+++ b/solution.py
@@ -9,6 +9,28 @@
 MOMENT = 0.9
 KEEP = 0.95
 NEG = -1e30
+
+
+def in_order(tiles, dim):
+    tiles = jnp.moveaxis(tiles, 0, dim)
+    shape = tiles.shape
+    return tiles.reshape(*shape[:dim], shape[dim] * shape[dim + 1], *shape[dim + 2 :])
+
+
+def ring_gather(x, axis, dim):
+    size = lax.axis_size(axis)
+    pairs = [(i, (i + 1) % size) for i in range(size)]
+    back = [(b, a) for a, b in pairs]
+    lower, upper = ([], [])
+    for step in range(size - 1):
+        if step % 2 == 0:
+            lower.append(lax.ppermute(lower[-1] if lower else x, axis, pairs))
+        else:
+            upper.append(lax.ppermute(upper[-1] if upper else x, axis, back))
+    parts = jnp.stack([*lower[::-1], x, *upper])
+    shift = lax.axis_index(axis) - len(lower)
+    parts = parts[(jnp.arange(size) - shift) % size]
+    return in_order(parts, dim)
 
 
 def layer_norm(values):
@@ -159,7 +181,7 @@
         lax.all_gather(low_weights[0], "fsdp", axis=0, tiled=True),
         lax.all_gather(low_weights[1], "fsdp", axis=1, tiled=True),
         lax.all_gather(low_weights[2], "fsdp", axis=0, tiled=True),
-        lax.all_gather(low_weights[3], "fsdp", axis=1, tiled=True),
+        ring_gather(low_weights[3], "fsdp", 1),
     )
     normed_one, factor_one = layer_norm(inputs)
     group_one = lax.all_gather(normed_one.astype(jnp.bfloat16), "seq", axis=0, tiled=True)

time: 1590 us -> 1690 us (1.063)
  waiting for transfers between devices: 1130 us -> 1180 us
  local copies, waits for them, and re-layouts: 78.1 us -> 100 us
  starting transfers between devices: 0.66 us -> 19.7 us
    ppermute x0 -> x7, waiting for transfers between devices: none -> 188 us  [the longest x4 182 us: ring_gather(): lower.append(lax.ppermute(lower[-1] if lower else x, axis, pairs))]
    all_gather x1, waiting for transfers between devices: 230 us -> 89.7 us  [on_device(): lax.all_gather(low_weights[2], 'fsdp', axis=0, tiled=True)]
    all_gather x1, waiting for transfers between devices: 94.6 us -> 125 us  [on_device(): lax.all_gather(low_weights[3], 'fsdp', axis=1, tiled=True)]
    all_gather x1, waiting for transfers between devices: 25.8 us -> 0.01 us  [on_device(): lax.all_gather(normed_two.astype(jnp.bfloat16), 'seq', axis=0, tiled=True)]
    ppermute x0 -> x7, starting transfers between devices: none -> 19 us  [the longest x3 15 us: ring_gather(): upper.append(lax.ppermute(upper[-1] if upper else x, axis, back))]
    unnamed x85 -> x101, local copies, waits for them, and re-layouts: 33 us -> 38.2 us
  transfers between devices with their start and end apart: 16 -> 23, of which waited for: 14 -> 18; matrix products, arithmetic and copies ran while one was open for 17% -> 16% of each run, Pallas kernels for 0% -> 0%
where the time goes in v1:
time: 1690 us
  waiting for transfers between devices  1180 us (70%)
  matrix products  222 us (13%)
  local copies, waits for them, and re-layouts  100 us (6%)
  other arithmetic  98.7 us (6%)
  blocking collectives  40.6 us (2%)
  starting transfers between devices  19.7 us (1%)
  between operations  17.2 us (1%)
    reduce_scatter x1, waiting for transfers between devices, on_device(): lax.psum_scatter(grad_gateup.astype(jnp.bfloat16), 'fsdp', scatter_dimens...  277 us
    ppermute x4, waiting for transfers between devices, ring_gather(): lower.append(lax.ppermute(lower[-1] if lower else x, axis, pairs))  182 us
    all_gather x1, waiting for transfers between devices, on_device(): lax.all_gather(low_weights[3], 'fsdp', axis=1, tiled=True)  125 us
    reduce_scatter x1, waiting for transfers between devices, on_device(): lax.psum_scatter(grad_qkv.astype(jnp.bfloat16), 'fsdp', scatter_dimension...  117 us
    all_gather x1, waiting for transfers between devices, on_device(): lax.all_gather(low_weights[0], 'fsdp', axis=0, tiled=True)  102 us
    all_gather x1, waiting for transfers between devices, on_device(): lax.all_gather(low_weights[2], 'fsdp', axis=0, tiled=True)  89.7 us
    reduce_scatter x1, waiting for transfers between devices, on_device(): lax.psum_scatter(normed_grad_two.astype(jnp.bfloat16), 'seq', scatter_dim...  44.7 us
    reduce_scatter x1, waiting for transfers between devices, on_device(): lax.psum_scatter(normed_grad_one.astype(jnp.bfloat16), 'seq', scatter_dim...  43.9 us
  transfers between devices with their start and end apart: 23, of which 18 were waited for; matrix products, arithmetic and copies ran while one was open for 16% of the time, Pallas kernels for 0%

profile of v1, /device:TPU:0, one launch (start us, length us, event | category | flops | bytes accessed | tf_op | source)
XLA Modules:
  0.0 1687.8 jit_solution(16341686114919573871)
XLA Ops:
  20.8 30.2 %all-gather.9.cloned.1.call-done = bf16[1024,2048]{1,0:T(8,128)(2,1)} async-done(((bf16[256,2048]{1,0:T(8,128)(2,1)}), bf16[1024,2048]{1,0:T(8,128)(2,1)}) %all-gather.9.cloned.1.call-update) | async-done | bytes 4194320 | tf_op jit(solution)/shard_map/all_gather | solution.py:187
  51.0 102.1 %all-gather.11.cloned.1.call-done = bf16[2048,3,512]{0,2,1:T(8,128)(2,1)} async-done(((bf16[256,3,512]{0,2,1:T(8,128)(2,1)}), bf16[2048,3,512]{0,2,1:T(8,128)(2,1)}) %all-gather.11.cloned.1.call-update) | async-done | bytes 6291472 | tf_op jit(solution)/shard_map/all_gather | solution.py:181
  177.2 24.9 %while.29 = (s32[]{:T(128)}, bf16[2,512,4,128]{3,1,2,0:T(8,128)(2,1)}, f32[2,4,512]{2,1,0:T(4,128)S(1)}, s32[2]{0:T(128)S(1)}, s32[]{:T(128)}, /*index=5*/bf16[1...) while((s32[]{:T(128)}, ...), condition=%wide.region_5.6_spmd.clone, body=%wide.region_2.5_spmd.sunk.clone | while | flops 1099955712 | bytes 31005332 | solution.py:91
  212.3 42.9 %reduce-scatter.9.cloned.1.call-done = bf16[256,2048]{1,0:T(8,128)(2,1)} async-done(((bf16[1024,2048]{1,0:T(8,128)(2,1)}), bf16[256,2048]{1,0:T(8,128)(2,1)}) %reduce-scatter.9.cloned.1.call-update) | async-done | bytes 1048592 | tf_op jit(solution)/shard_map/reduce_scatter | solution.py:198
  269.3 26.0 %collective-permute-done = bf16[2048,256]{1,0:T(8,128)(2,1)S(1)} collective-permute-done((bf16[2048,256]{1,0:T(8,128)(2,1)S(1)}, bf16[2048,256]{1,0:T(8,128)(2,1)S(1)}, u32[]{:S(2)}, u32[]{:S(2)}) %collective-permute-start) | collective-permute-done | bytes 1048608 | tf_op jit(solution)/shard_map/ppermute | solution.py:27
  300.0 62.6 %collective-permute-done.1 = bf16[2048,256]{1,0:T(8,128)(2,1)S(1)} collective-permute-done((bf16[2048,256]{1,0:T(8,128)(2,1)S(1)}, bf16[2048,256]{1,0:T(8,128)(2,1)S(1)}, u32[]{:S(2)}, u32[]{:S(2)}) %collective-permute-start.1) | collective-permute-done | bytes 1048608 | tf_op jit(solution)/shard_map/ppermute | solution.py:27
  370.2 40.1 %collective-permute-done.2 = bf16[2048,256]{1,0:T(8,128)(2,1)} collective-permute-done((bf16[2048,256]{1,0:T(8,128)(2,1)S(1)}, bf16[2048,256]{1,0:T(8,128)(2,1)}, u32[]{:S(2)}, u32[]{:S(2)}) %collective-permute-start.2) | collective-permute-done | bytes 1048608 | tf_op jit(solution)/shard_map/ppermute | solution.py:27
  421.2 53.5 %collective-permute-done.3 = bf16[2048,256]{1,0:T(8,128)(2,1)} collective-permute-done((bf16[2048,256]{1,0:T(8,128)(2,1)}, bf16[2048,256]{1,0:T(8,128)(2,1)}, u32[]{:S(2)}, u32[]{:S(2)}) %collective-permute-start.3) | collective-permute-done | bytes 1048608 | tf_op jit(solution)/shard_map/ppermute | solution.py:27
  507.9 89.7 %all-gather.17.cloned.1.call-done = bf16[2048,2,2048]{2,0,1:T(8,128)(2,1)} async-done(((bf16[256,2,2048]{2,0,1:T(8,128)(2,1)}), bf16[2048,2,2048]{2,0,1:T(8,128)(2,1)}) %all-gather.17.cloned.1.call-update) | async-done | bytes 16777232 | tf_op jit(solution)/shard_map/all_gather | solution.py:183
  597.6 23.5 %fusion.52 = f32[1024,2,2048]{2,0,1:T(8,128)} fusion(bf16[2048,2,2048]{2,0,1:T(8,128)(2,1)} %all-gather.17.cloned.1.call-done, bf16[1024,2048]{1,0:T(8,128)(2,1)} %all-gather.15.cloned.1.call-done), kind=kOutput, calls=%fused_computation.81 | convolution fusion | flops 17179869184 | bytes 37748736 | tf_op jit(solution)/shard_map/td,djf->tjf/dot_general | solution.py:203
  621.0 17.5 %fusion.61 = bf16[1024,2048]{1,0:T(8,128)(2,1)} fusion(bf16[2048,2048]{0,1:T(8,128)(2,1)} %bitcast.264, f32[1024,2,2048]{2,0,1:T(8,128)} %fusion.52), kind=kOutput, calls=%fused_computation.92 | convolution fusion | flops 8604614656 | bytes 29360128 | tf_op jit(solution)/shard_map/dot_general | solution.py:207
  641.3 41.6 %reduce-scatter.11.cloned.1.call-done = bf16[256,2048]{1,0:T(8,128)(2,1)} async-done(((bf16[1024,2048]{1,0:T(8,128)(2,1)}), bf16[256,2048]{1,0:T(8,128)(2,1)}) %reduce-scatter.11.cloned.1.call-update) | async-done | bytes 1048592 | tf_op jit(solution)/shard_map/reduce_scatter | solution.py:208
  686.0 124.5 %all-gather.21.cloned.1.call-done = bf16[2048,2048]{1,0:T(8,128)(2,1)} async-done(((bf16[2048,256]{1,0:T(8,128)(2,1)}), bf16[2048,2048]{1,0:T(8,128)(2,1)}) %all-gather.21.cloned.1.call-update) | async-done | bytes 8388624 | tf_op jit(solution)/shard_map/all_gather | solution.py:218
  810.5 34.8 %all-gather.19.cloned.1.call-done = bf16[1024,2048]{1,0:T(8,128)(2,1)} async-done(((bf16[256,2048]{1,0:T(8,128)(2,1)}), bf16[1024,2048]{1,0:T(8,128)(2,1)}) %all-gather.19.cloned.1.call-update) | async-done | bytes 4194320 | tf_op jit(solution)/shard_map/all_gather | solution.py:222
  845.4 20.5 %fusion.60 = (bf16[1024,1,2048]{2,0,1:T(8,128)(2,1)}, bf16[1024,1,2048]{2,0,1:T(8,128)(2,1)}) fusion(f32[1024,2,2048]{2,0,1:T(8,128)} %fusion.52, bf16[1024,2048]{1,0:T(8,128)(2,1)} %all-gather.19.cloned.1.call-done, bf16[2048,2048]{1,0:T(8,128)(2,1)} %all-gather.21.cloned.1.call-done), kind=kOutput, calls=%fused_computation.90 | convolution fusion | flops 8617197568 | bytes 37748736 | tf_op jit(solution)/shard_map/dot_general | solution.py:223
  865.9 23.8 %bitcast_convert_fusion.1 = bf16[1024,2048]{1,0:T(8,128)(2,1)} fusion(bf16[2048,2,2048]{2,0,1:T(8,128)(2,1)} %all-gather.17.cloned.1.call-done, bf16[1024,1,2048]{2,0,1:T(8,128)(2,1)} %get-tuple-element.321, bf16[1024,1,2048]{2,0,1:T(8,128)(2,1)} %get-tuple-element.320), kind=kOutput, calls=%fused_computation.53 | convolution fusion | flops 17186160640 | bytes 29360128 | tf_op jit(solution)/shard_map/tjf,djf->td/dot_general | solution.py:231
  889.7 44.7 %reduce-scatter.13.cloned.1.call-done = bf16[256,2048]{1,0:T(8,128)(2,1)} async-done(((bf16[1024,2048]{1,0:T(8,128)(2,1)}), bf16[256,2048]{1,0:T(8,128)(2,1)}) %reduce-scatter.13.cloned.1.call-update) | async-done | bytes 1048592 | tf_op jit(solution)/shard_map/reduce_scatter | solution.py:235
  988.6 52.2 %while.30 = (s32[]{:T(128)}, f32[1024,4,128]{0,2,1:T(8,128)S(1)}, f32[1024,4,128]{0,2,1:T(8,128)}, f32[2,512,4,128]{3,1,2,0:T(8,128)}, s32[2]{0:T(128)S(1)}, /*i...) while((s32[]{:T(128)}, f32[1024,4,128]{0,2,1:T(8,128)S(1)}, ...), condition=%wide.region_16.17_spmd.clone.clone, body=%wide.region_14.16_spmd.clone.sunk.clone | while | flops 2719743488 | bytes 180419536 | solution.py:131
  1096.1 24.7 %convolution_convert_fusion = bf16[2048,2,2048]{2,0,1:T(8,128)(2,1)} fusion(bf16[1024,1,2048]{2,0,1:T(8,128)(2,1)} %get-tuple-element.321, bf16[1024,1,2048]{2,0,1:T(8,128)(2,1)} %get-tuple-element.320, bf16[1024,2048]{1,0:T(8,128)(2,1)} %all-gather.15.cloned.1.call-done), kind=kOutput, calls=%fused_computation.50 | convolution fusion | flops 17205035008 | bytes 29360128 | tf_op jit(solution)/shard_map/td,tjf->djf/dot_general | solution.py:234
  1120.8 40.6 %psum.7 = f32[]{:T(128)} all-reduce(f32[]{:T(128)} %get-tuple-element.260), channel_id=1, replica_groups=mesh['seq'=4,'fsdp'=8] {'seq','fsdp'}, use_global_device_ids=true, to_apply=%region_21.22 | all-reduce | flops 1 | bytes 8 | tf_op jit(solution)/shard_map/psum | solution.py:212
  1167.9 31.7 %reduce-scatter.19.cloned.1.call-done = bf16[512,256]{1,0:T(8,128)(2,1)} async-done(((bf16[512,2048]{1,0:T(8,128)(2,1)}), bf16[512,256]{1,0:T(8,128)(2,1)}) %reduce-scatter.19.cloned.1.call-update) | async-done | bytes 262160 | tf_op jit(solution)/shard_map/reduce_scatter | solution.py:270
  1202.3 43.9 %reduce-scatter.15.cloned.1.call-done = bf16[256,2048]{1,0:T(8,128)(2,1)} async-done(((bf16[1024,2048]{1,0:T(8,128)(2,1)}), bf16[256,2048]{1,0:T(8,128)(2,1)}) %reduce-scatter.15.cloned.1.call-update) | async-done | bytes 1048592 | tf_op jit(solution)/shard_map/reduce_scatter | solution.py:262
  1251.2 117.0 %reduce-scatter.17.cloned.1.call-done = bf16[256,3,512]{2,0,1:T(8,128)(2,1)} async-done(((bf16[2048,3,512]{2,0,1:T(8,128)(2,1)}), bf16[256,3,512]{2,0,1:T(8,128)(2,1)}) %reduce-scatter.17.cloned.1.call-update) | async-done | bytes 786448 | tf_op jit(solution)/shard_map/reduce_scatter | solution.py:267
  1373.6 276.9 %reduce-scatter.21.cloned.1.call-done = bf16[256,2,2048]{2,0,1:T(8,128)(2,1)} async-done(((bf16[2048,2,2048]{2,0,1:T(8,128)(2,1)}), bf16[256,2,2048]{2,0,1:T(8,128)(2,1)}) %reduce-scatter.21.cloned.1.call-update) | async-done | bytes 2097168 | tf_op jit(solution)/shard_map/reduce_scatter | solution.py:273
  (293 shorter events, 349.4 us)
Async XLA Ops:
  7.2 43.8 %all-gather.9.cloned.1.call-start = ((), (), s32[]{:S(2)}) async-start(), calls=%async_computation.8 | async-start | bytes 5242880 | tf_op jit(solution)/shard_map/all_gather | solution.py:187
  13.7 139.5 %all-gather.11.cloned.1.call-start = ((), (), s32[]{:S(2)}) async-start(), calls=%async_computation.9 | async-start | bytes 7077888 | tf_op jit(solution)/shard_map/all_gather | solution.py:181
  14.9 191.1 %all-gather.13.cloned.1.call-start = ((), (), s32[]{:S(2)}) async-start(), calls=%async_computation.10 | async-start | bytes 2359296 | tf_op jit(solution)/shard_map/all_gather | solution.py:182
  15.7 239.5 %reduce-scatter.9.cloned.1.call-start = ((), (), s32[]{:S(2)}) async-start(), calls=%async_computation.11 | async-start | bytes 5242880 | tf_op jit(solution)/shard_map/reduce_scatter | solution.py:198
  212.3 295.6 %all-gather.15.cloned.1.call-start = ((), (), s32[]{:S(2)}) async-start(), calls=%async_computation.12 | async-start | bytes 5242880 | tf_op jit(solution)/shard_map/all_gather | solution.py:202
  260.0 337.5 %all-gather.17.cloned.1.call-start = ((), (), s32[]{:S(2)}) async-start(), calls=%async_computation.13 | async-start | bytes 18874368 | tf_op jit(solution)/shard_map/all_gather | solution.py:183
  265.9 417.1 %reduce-scatter.11.cloned.1.call-start = ((), (), s32[]{:S(2)}) async-start(), calls=%async_computation.14 | async-start | bytes 5242880 | tf_op jit(solution)/shard_map/reduce_scatter | solution.py:208
  267.8 212.6 %copy-start.31 = (bf16[2048,256]{1,0:T(8,128)(2,1)}, bf16[2048,256]{1,0:T(8,128)(2,1)S(1)}, u32[]{:S(2)}) copy-start(bf16[2048,256]{1,0:T(8,128)(2,1)S(1)} %convert_element_type.154) | copy-start | bytes 3145732
  267.8 27.5 %collective-permute-start = (bf16[2048,256]{1,0:T(8,128)(2,1)S(1)}, bf16[2048,256]{1,0:T(8,128)(2,1)S(1)}, u32[]{:S(2)}, u32[]{:S(2)}) collective-permute-start(bf16[2048,256]{1,0:T(8,128)(2,1)S(1)} %convert_element_type.154), channel_id=1, source_target_pairs={{0,1},{1,2},{2,3},{3,4},{4,5},{5,6},{6,7},{7,0},{8,9},{9,10},{10,1... | collective-permute-start | bytes 3145736 | tf_op jit(solution)/shard_map/ppermute | solution.py:27
  295.3 67.3 %collective-permute-start.1 = (bf16[2048,256]{1,0:T(8,128)(2,1)S(1)}, bf16[2048,256]{1,0:T(8,128)(2,1)S(1)}, u32[]{:S(2)}, u32[]{:S(2)}) collective-permute-start(bf16[2048,256]{1,0:T(8,128)(2,1)S(1)} %collective-permute-done), channel_id=1, source_target_pairs={{0,1},{1,2},{2,3},{3,4},{4,5},{5,6},{6,7},{7,0},{8,9},{9,10},{10,1... | collective-permute-start | bytes 3145736 | tf_op jit(solution)/shard_map/ppermute | solution.py:27
  295.3 69.8 %collective-permute-start.4 = (bf16[2048,256]{1,0:T(8,128)(2,1)S(1)}, bf16[2048,256]{1,0:T(8,128)(2,1)}, u32[]{:S(2)}, u32[]{:S(2)}) collective-permute-start(bf16[2048,256]{1,0:T(8,128)(2,1)S(1)} %convert_element_type.154), channel_id=1, source_target_pairs={{1,0},{2,1},{3,2},{4,3},{5,4},{6,5},{7,6},{0,7},{9,8},{10,9},{11,1... | collective-permute-start | bytes 3145736 | tf_op jit(solution)/shard_map/ppermute | solution.py:29
  362.6 47.7 %collective-permute-start.2 = (bf16[2048,256]{1,0:T(8,128)(2,1)S(1)}, bf16[2048,256]{1,0:T(8,128)(2,1)}, u32[]{:S(2)}, u32[]{:S(2)}) collective-permute-start(bf16[2048,256]{1,0:T(8,128)(2,1)S(1)} %collective-permute-done.1), channel_id=1, source_target_pairs={{0,1},{1,2},{2,3},{3,4},{4,5},{5,6},{6,7},{7,0},{8,9},{9,10},{10,1... | collective-permute-start | bytes 3145736 | tf_op jit(solution)/shard_map/ppermute | solution.py:27
  365.1 50.9 %collective-permute-start.5 = (bf16[2048,256]{1,0:T(8,128)(2,1)}, bf16[2048,256]{1,0:T(8,128)(2,1)}, u32[]{:S(2)}, u32[]{:S(2)}) collective-permute-start(bf16[2048,256]{1,0:T(8,128)(2,1)} %collective-permute-done.4), channel_id=1, source_target_pairs={{1,0},{2,1},{3,2},{4,3},{5,4},{6,5},{7,6},{0,7},{9,8},{10,9},{11,1... | collective-permute-start | bytes 3145736 | tf_op jit(solution)/shard_map/ppermute | solution.py:29
  410.3 64.4 %collective-permute-start.3 = (bf16[2048,256]{1,0:T(8,128)(2,1)}, bf16[2048,256]{1,0:T(8,128)(2,1)}, u32[]{:S(2)}, u32[]{:S(2)}) collective-permute-start(bf16[2048,256]{1,0:T(8,128)(2,1)} %collective-permute-done.2), channel_id=1, source_target_pairs={{0,1},{1,2},{2,3},{3,4},{4,5},{5,6},{6,7},{7,0},{8,9},{9,10},{10,1... | collective-permute-start | bytes 3145736 | tf_op jit(solution)/shard_map/ppermute | solution.py:27
  416.0 71.2 %collective-permute-start.6 = (bf16[2048,256]{1,0:T(8,128)(2,1)}, bf16[2048,256]{1,0:T(8,128)(2,1)S(1)}, u32[]{:S(2)}, u32[]{:S(2)}) collective-permute-start(bf16[2048,256]{1,0:T(8,128)(2,1)} %collective-permute-done.5), channel_id=1, source_target_pairs={{1,0},{2,1},{3,2},{4,3},{5,4},{6,5},{7,6},{0,7},{9,8},{10,9},{11,1... | collective-permute-start | bytes 3145736 | tf_op jit(solution)/shard_map/ppermute | solution.py:29
  638.5 172.0 %all-gather.21.cloned.1.call-start = ((), (), s32[]{:S(2)}) async-start(), calls=%async_computation.16 | async-start | bytes 9437184 | tf_op jit(solution)/shard_map/all_gather | solution.py:218
  639.3 206.1 %all-gather.19.cloned.1.call-start = ((), (), s32[]{:S(2)}) async-start(), calls=%async_computation.15 | async-start | bytes 5242880 | tf_op jit(solution)/shard_map/all_gather | solution.py:222
  686.0 248.4 %reduce-scatter.13.cloned.1.call-start = ((), (), s32[]{:S(2)}) async-start(), calls=%async_computation.17 | async-start | bytes 5242880 | tf_op jit(solution)/shard_map/reduce_scatter | solution.py:235
  889.7 86.7 %all-gather.23.cloned.1.call-start = ((), (), s32[]{:S(2)}) async-start(), calls=%async_computation.18 | async-start | bytes 5242880 | tf_op jit(solution)/shard_map/all_gather | solution.py:239
  941.8 220.3 %reduce-scatter.23.cloned.1.call-start = ((), (), s32[]{:S(2)}) async-start(), calls=%async_computation.23 | async-start | bytes 9437184 | tf_op jit(solution)/shard_map/reduce_scatter | solution.py:276
  958.4 241.2 %reduce-scatter.19.cloned.1.call-start = ((), (), s32[]{:S(2)}) async-start(), calls=%async_computation.21 | async-start | bytes 2359296 | tf_op jit(solution)/shard_map/reduce_scatter | solution.py:270
  982.3 263.9 %reduce-scatter.15.cloned.1.call-start = ((), (), s32[]{:S(2)}) async-start(), calls=%async_computation.19 | async-start | bytes 5242880 | tf_op jit(solution)/shard_map/reduce_scatter | solution.py:262
  1083.0 285.1 %reduce-scatter.17.cloned.1.call-start = ((), (), s32[]{:S(2)}) async-start(), calls=%async_computation.20 | async-start | bytes 7077888 | tf_op jit(solution)/shard_map/reduce_scatter | solution.py:267
  1096.0 554.4 %reduce-scatter.21.cloned.1.call-start = ((), (), s32[]{:S(2)}) async-start(), calls=%async_computation.22 | async-start | bytes 18874368 | tf_op jit(solution)/shard_map/reduce_scatter | solution.py:273
  (60 other events, 884.2 us)
Sparse Core Ops, SparseCore 0:
  13.8 37.1 all-gather.8
  53.6 99.4 all-gather.10
  155.7 48.5 all-gather.12
  212.4 42.7 reduce-scatter.8
  260.2 34.4 all-gather.14
  297.3 300.2 all-gather.16
  638.6 44.2 reduce-scatter.10
  685.6 124.9 all-gather.20
  812.7 32.6 all-gather.18
  889.8 44.5 reduce-scatter.12
  941.9 34.4 all-gather.22
  979.9 147.8 reduce-scatter.22
  1131.3 68.2 reduce-scatter.18
  1202.6 43.5 reduce-scatter.14
  1249.7 118.4 reduce-scatter.16
  1371.7 278.6 reduce-scatter.20
